TPU v7x, 32 devices: a whole 2x2x4 slice. The times are simulated.
32 devices in a mesh: rep: 4 (over x, core), grp: 8 (over z, y).
Axes of the slice: x: 2, y: 2, z: 4, core: 2. Of those that a mesh axis runs over, the one named last changes fastest.
Arguments:
- tokens: bfloat16 [8192, 2304], P(('rep', 'grp')), may hold values from -6 to 6
- norm_gain: float32 [2304], replicated, may hold values from 0.25 to 1.75
- key_weight: bfloat16 [2304, 1024], P('grp'), may hold values from -0.125 to 0.125
- key_grad: bfloat16 [8192, 1024], P(('rep', 'grp')), may hold values from -6 to 6
Outputs:
- token_grad: bfloat16 [8192, 2304], P(('rep', 'grp'))
- weight_grad: float32 [2304, 1024], P('grp', 'rep')
- gain_grad: float32 [2304], replicated
All inputs are finite; a program needn't handle non-finite values.
Results may differ from a plain program's by a relative error of at most 0.023.
Values may be sent and summed in bfloat16 or wider, within the bound.
A program may use at most 64 MiB of HBM per device.

v0:
```python
import functools

import jax
import jax.numpy as jnp
from jax import lax
from jax.experimental import pallas as pl
from jax.experimental.pallas import tpu as pltpu
from jax.sharding import PartitionSpec as P

epsilon = 1e-06
MESH = pl.DeviceIdType.MESH
LANES = 128


def flip(i, bits):
    bit = 1
    while bit <= bits:
        if bits & bit:
            i = i + bit * (1 - 2 * lax.rem(lax.div(i, bit), 2))
        bit *= 2
    return i


def kernel(
    n_z, grad_scale,
    tok_hbm, gain_hbm, w_ref, kg_hbm,
    tg_ref, wg_ref, gg_ref,
    tok_ref, gain_ref, kg_ref, load_sem, wfull, normed_t, dn, mine, give, take, in1, in2, in3, gsend, grecv,
    w_send, w_recv, c_send, c_recv, s1_send, s1_recv, s2_send, s2_recv, s3_send, s3_recv, g_send, g_recv,
):
    rep, grp = lax.axis_index("rep"), lax.axis_index("grp")
    x, c = lax.div(rep, 2), lax.rem(rep, 2)
    z, y = lax.div(grp, 2), lax.rem(grp, 2)
    rows, keys = w_ref.shape
    features = tok_ref.shape[1]
    cols = mine.shape[-1]
    peer_c = (2 * x + 1 - c, grp)
    peer_x = (2 * (1 - x) + c, grp)
    peer_cx = (2 * (1 - x) + 1 - c, grp)
    peer_y = (rep, 2 * z + 1 - y)
    peer_z = [None] + [(rep, 2 * flip(z, k) + y) for k in range(1, n_z)]
    group = [peer_y]
    for k in range(1, n_z):
        group += [peer_z[k], (rep, 2 * flip(z, k) + 1 - y)]

    def row_at(k, yy):
        g = 2 * flip(z, k) + (1 - y if yy else y)
        return pl.ds(pl.multiple_of(g * rows, 16), rows)

    loads = [
        pltpu.make_async_copy(src, dst, load_sem.at[n])
        for n, (src, dst) in enumerate(
            ((tok_hbm, tok_ref), (gain_hbm, gain_ref), (kg_hbm, kg_ref), (w_ref, wfull.at[row_at(0, 0), :]))
        )
    ]
    for load in loads:
        load.start()

    barrier = pltpu.get_barrier_semaphore()
    peers = [peer_c, peer_x, peer_cx] + group
    for peer in peers:
        pl.semaphore_signal(barrier, inc=1, device_id=peer, device_id_type=MESH)
    pl.semaphore_wait(barrier, len(peers))

    sends = []

    def send(src, dst, s_sem, r_sem, peer):
        copy = pltpu.make_async_remote_copy(
            src_ref=src, dst_ref=dst, send_sem=s_sem, recv_sem=r_sem, device_id=peer, device_id_type=MESH
        )
        copy.start()
        sends.append(copy)

    def arrived(dst, sem):
        pltpu.make_async_remote_copy(
            src_ref=dst, dst_ref=dst, send_sem=sem, recv_sem=sem, device_id=peer_c, device_id_type=MESH
        ).wait_recv()

    def col_at(xx, cc):
        r = 2 * (1 - x if xx else x) + (1 - c if cc else c)
        return pl.ds(pl.multiple_of(r * cols, LANES), cols)

    def piece(xx, cc, k, yy):
        return wfull.at[row_at(k, yy), col_at(xx, cc)]

    def got(xx, cc, k, yy):
        arrived(piece(xx, cc, k, yy), w_recv.at[xx, cc, k, yy])

    def w_fwd(axis, xx, k, yy):
        there = {0: (xx, 1, k, yy), 1: (1 - xx, 0, k, yy), 2: (xx, 0, k, 1 - yy)}[axis]
        peer = (peer_c, peer_x, peer_y)[axis]
        ref = piece(xx, 0, k, yy)
        send(ref, ref, w_send.at[axis, xx, k, yy], w_recv.at[there], peer)

    def own_to(axis, xx, k, peer):
        there = (xx, 0, 0, 1) if axis == 2 else (xx, 0, k, 0)
        send(
            w_ref.at[:, col_at(xx, 0)], piece(xx, 0, 0, 0), w_send.at[axis, xx, k, 0], w_recv.at[there], peer
        )

    own_to(2, 0, 0, peer_y)
    for k in range(1, n_z):
        own_to(3, 0, k, peer_z[k])
    own_to(2, 1, 0, peer_y)
    for k in range(1, n_z - 1):
        own_to(3, 1, k, peer_z[k])

    loads[0].wait()
    acc = None
    for j in range(features // LANES):
        t = tok_ref[:, j * LANES:(j + 1) * LANES].astype(jnp.float32)
        acc = t * t if acc is None else acc + t * t
    inv = lax.rsqrt(jnp.sum(acc, axis=1, keepdims=True) / features + epsilon)
    loads[1].wait()
    for j in range(features // LANES):
        at = slice(j * LANES, (j + 1) * LANES)
        t = tok_ref[:, at].astype(jnp.float32)
        normed_t[at, :] = (t * inv * gain_ref[at].reshape(1, -1)).T.astype(jnp.bfloat16)

    def partial(k):
        for cc in (1, 0):
            for yy in (0, 1):
                for xx in (0, 1):
                    block = jnp.dot(
                        normed_t[row_at(k, yy), :], kg_ref[:, col_at(xx, cc)], preferred_element_type=jnp.float32
                    ).astype(jnp.bfloat16)
                    (give if cc else mine)[k, yy, xx] = block
            if cc:
                send(give.at[k], take.at[k], c_send.at[k], c_recv.at[k], peer_c)

    def add(k, yy, xx, ref):
        mine[k, yy, xx] = (
            mine[k, yy, xx].astype(jnp.float32) + ref[...].astype(jnp.float32)
        ).astype(jnp.bfloat16)

    def x_first(k):
        return k % 2 == 1

    def core_in(k):
        arrived(take.at[k], c_recv.at[k])

    def stage1(k, slot):
        for other in (1, 0):
            yy, xx = (slot, other) if x_first(k) else (other, slot)
            add(k, yy, xx, take.at[k, yy, xx])
            if other:
                send(
                    mine.at[k, yy, xx], in1.at[k, slot], s1_send.at[k, slot], s1_recv.at[k, slot],
                    peer_x if x_first(k) else peer_y,
                )

    def stage2(k, slot):
        arrived(in1.at[k, slot], s1_recv.at[k, slot])
        yy, xx = (slot, 0) if x_first(k) else (0, slot)
        add(k, yy, xx, in1.at[k, slot])
        if slot:
            send(mine.at[k, yy, xx], in2.at[k], s2_send.at[k], s2_recv.at[k], peer_y if x_first(k) else peer_x)

    def stage3(k):
        arrived(in2.at[k], s2_recv.at[k])
        add(k, 0, 0, in2.at[k])
        send(mine.at[k, 0, 0], in3.at[k], s3_send.at[k], s3_recv.at[k], peer_z[k])

    def take_on(xx, k, yy, *axes):
        got(xx, 0, k, yy)
        for axis in axes + (0,):
            w_fwd(axis, xx, k, yy)

    loads[2].wait()
    partial(3)
    take_on(0, 1, 0, 2)
    partial(2)
    core_in(3)
    stage1(3, 1)
    stage1(3, 0)
    take_on(0, 2, 0, 2)
    core_in(2)
    stage1(2, 1)
    stage1(2, 0)
    take_on(0, 0, 1)
    take_on(0, 1, 1, 1)
    partial(1)
    partial(0)
    take_on(0, 2, 1, 1)
    stage2(3, 1)
    take_on(0, 3, 0, 1, 2)
    core_in(1)
    core_in(0)
    stage2(3, 0)
    take_on(1, 0, 1)
    take_on(1, 1, 0)
    stage2(2, 1)
    take_on(1, 1, 1)
    stage1(1, 1)
    stage1(0, 1)
    stage1(0, 0)
    take_on(1, 2, 1)
    take_on(0, 3, 1, 1)
    stage1(1, 0)
    take_on(1, 2, 0)
    stage2(2, 0)
    take_on(1, 3, 0)
    stage3(3)
    stage3(2)
    stage2(1, 1)
    stage2(0, 1)
    take_on(1, 3, 1)
    loads[3].wait()
    for k in range(n_z):
        for yy in (0, 1):
            for xx in (0, 1):
                if k or yy:
                    got(xx, 1, k, yy)

    wide = 2 * LANES
    inner = jnp.zeros((tok_ref.shape[0], LANES), jnp.float32)
    for j in range(features // wide):
        at = slice(j * wide, (j + 1) * wide)
        d = lax.dot_general(
            kg_ref[...], wfull[at, :], (((1,), (1,)), ((), ())), preferred_element_type=jnp.float32
        )
        dn[:, at] = d
        dt = d * tok_ref[:, at].astype(jnp.float32)
        gsend[0, :, at] = jnp.sum(dt * inv, axis=0, keepdims=True)
        scaled = dt * gain_ref[at].reshape(1, -1)
        inner = inner + scaled[:, :LANES] + scaled[:, LANES:]
    for n, peer in enumerate((peer_c, peer_x, peer_cx)):
        send(gsend.at[0], grecv.at[n], g_send.at[n], g_recv.at[n], peer)
    for k in (1, 0):
        stage2(k, 0)
    stage3(1)
    mean = jnp.sum(inner, axis=1, keepdims=True) / features
    pull = inv * inv * mean

    def token_grad(lo, hi):
        for j in range(lo, hi):
            at = slice(j * wide, (j + 1) * wide)
            t = tok_ref[:, at].astype(jnp.float32)
            tg_ref[:, at] = (inv * (dn[:, at] * gain_ref[at].reshape(1, -1) - t * pull)).astype(jnp.bfloat16)

    steps = features // wide
    token_grad(0, steps // 3)
    for n in range(3):
        arrived(grecv.at[n], g_recv.at[n])
    gsend[1] = (gsend[0] + grecv[0]) + (grecv[1] + grecv[2])
    for n, peer in enumerate(group):
        send(gsend.at[1], grecv.at[3 + n], g_send.at[3 + n], g_recv.at[3 + n], peer)
    token_grad(steps // 3, steps)

    arrived(in2.at[0], s2_recv.at[0])
    total = mine[0, 0, 0].astype(jnp.float32) + in2[0].astype(jnp.float32)
    for k in range(1, n_z):
        arrived(in3.at[k], s3_recv.at[k])
        total = total + in3[k].astype(jnp.float32)
    wg_ref[...] = total * grad_scale

    terms = [gsend[1]]
    for n in range(3, 3 + len(group)):
        arrived(grecv.at[n], g_recv.at[n])
        terms.append(grecv[n])
    while len(terms) > 1:
        terms = [terms[i] + terms[i + 1] for i in range(0, len(terms), 2)]
    total = terms[0] * grad_scale
    for j in range(features // LANES):
        at = slice(j * LANES, (j + 1) * LANES)
        gg_ref[at] = total[:, at].reshape(LANES)
    for copy in sends:
        copy.wait_send()


def fused(n_rep, n_grp, tokens, norm_gain, key_weight, key_grad):
    n_tok, features = tokens.shape
    rows, keys = key_weight.shape
    cols, n_z = keys // n_rep, n_grp // 2
    grad_scale = (n_tok * n_rep * n_grp) ** (-0.5)
    vmem = pl.BlockSpec(memory_space=pltpu.VMEM)
    bf16, f32, dma = jnp.bfloat16, jnp.float32, pltpu.SemaphoreType.DMA
    block = (rows, cols)
    token_grad, weight_grad, gain_grad = pl.pallas_call(
        functools.partial(kernel, n_z, grad_scale),
        out_shape=(
            jax.ShapeDtypeStruct((n_tok, features), bf16),
            jax.ShapeDtypeStruct(block, f32),
            jax.ShapeDtypeStruct((features,), f32),
        ),
        in_specs=[pl.BlockSpec(memory_space=pl.ANY)] * 4,
        out_specs=(vmem,) * 3,
        scratch_shapes=[
            pltpu.VMEM((n_tok, features), bf16),
            pltpu.VMEM((features,), f32),
            pltpu.VMEM((n_tok, keys), bf16),
            dma((4,)),
            pltpu.VMEM((features, keys), bf16),
            pltpu.VMEM((features, n_tok), bf16),
            pltpu.VMEM((n_tok, features), f32),
            pltpu.VMEM((n_z, 2, 2) + block, bf16),
            pltpu.VMEM((n_z, 2, 2) + block, bf16),
            pltpu.VMEM((n_z, 2, 2) + block, bf16),
            pltpu.VMEM((n_z, 2) + block, bf16),
            pltpu.VMEM((n_z,) + block, bf16),
            pltpu.VMEM((n_z,) + block, bf16),
            pltpu.VMEM((2, 1, features), f32),
            pltpu.VMEM((2 * n_z + 2, 1, features), f32),
            dma((4, 2, n_z, 2)), dma((2, 2, n_z, 2)),
            dma((n_z,)), dma((n_z,)),
            dma((n_z, 2)), dma((n_z, 2)),
            dma((n_z,)), dma((n_z,)),
            dma((n_z,)), dma((n_z,)),
            dma((2 * n_z + 2,)), dma((2 * n_z + 2,)),
        ],
        compiler_params=pltpu.CompilerParams(
            collective_id=0, has_side_effects=True, vmem_limit_bytes=60 * 1024 * 1024
        ),
    )(tokens, norm_gain, key_weight, key_grad)
    return token_grad, weight_grad, gain_grad


def plain(tokens, norm_gain, key_weight, key_grad):
    total_tokens = tokens.shape[0] * lax.axis_size("rep") * lax.axis_size("grp")
    grad_scale = total_tokens ** (-0.5)
    wide_tokens = tokens.astype(jnp.float32)
    inv_rms = lax.rsqrt(jnp.mean(wide_tokens * wide_tokens, axis=1, keepdims=True) + epsilon)
    normed = (wide_tokens * inv_rms * norm_gain).astype(jnp.bfloat16)
    partial_value = lax.dot_general(
        normed, key_grad, (((0,), (0,)), ((), ())), preferred_element_type=jnp.float32
    )
    d_normed = lax.dot_general(
        key_grad,
        lax.all_gather(key_weight, "grp", axis=0, tiled=True),
        (((1,), (1,)), ((), ())),
        preferred_element_type=jnp.float32,
    )
    section_one = lax.psum_scatter(
        partial_value.astype(jnp.bfloat16), "rep", scatter_dimension=1, tiled=True
    ).astype(jnp.float32)
    weight_sum = lax.psum_scatter(section_one, "grp", scatter_dimension=0, tiled=True)
    gain_local = jnp.sum(d_normed * wide_tokens * inv_rms, axis=0)
    gain_total = lax.psum(gain_local, ("rep", "grp"))
    scaled = d_normed * norm_gain
    inner_mean = jnp.mean(scaled * wide_tokens, axis=1, keepdims=True)
    token_grad = (inv_rms * (scaled - wide_tokens * inv_rms * inv_rms * inner_mean)).astype(
        jnp.bfloat16
    )
    return (token_grad, weight_sum * grad_scale, gain_total * grad_scale)


def shards(tokens, norm_gain, key_weight, key_grad):
    n_rep, n_grp = lax.axis_size("rep"), lax.axis_size("grp")
    n_z = n_grp // 2
    if (
        n_rep == 2 * 2 and n_grp == 2 * 4
        and key_weight.shape[1] % (n_rep * LANES) == 0 and key_weight.shape[0] % 16 == 0
        and tokens.shape[1] % (2 * LANES) == 0 and tokens.shape[0] % LANES == 0
    ):
        return fused(n_rep, n_grp, tokens, norm_gain, key_weight, key_grad)
    return plain(tokens, norm_gain, key_weight, key_grad)


def solution(mesh):
    in_specs = (P(("rep", "grp"), None), P(), P("grp", None), P(("rep", "grp"), None))
    out_specs = (P(("rep", "grp"), None), P("grp", "rep"), P())
    return jax.shard_map(shards, mesh=mesh, in_specs=in_specs, out_specs=out_specs, check_vma=False)
```

profile of v0, /device:TPU:0, one launch (start us, length us, event | category | flops | bytes accessed | tf_op | source)
XLA Modules:
  0.0 59.8 jit_solution(8925108120913528559)
XLA Ops:
  0.6 55.4 %shard_map.67 = (bf16[256,2304]{1,0:T(8,128)(2,1)}, f32[288,256]{1,0:T(8,128)}, f32[2304]{0:T(1024)}) custom-call(bf16[256,2304]{1,0:T(8,128)(2,1)} %tok_hbm.1, f32[2304]{0:T(1024)} %gain_hbm.1, bf16[288,1024]{1,0:T(8,128)(2,1)} %w_ref.1, bf16[256,1024]{1,0:T(8,128)(2,1)} %kg_hbm.1), custom_call_target="tpu_custom_call" | custom-call | tf_op jit(solution)/shard_map/pallas_call | solution.py:279
  56.0 0.0 copy-start
  56.0 0.0 copy-start.1
  56.0 2.4 %copy.10 = bf16[256,2304]{1,0:T(8,128)(2,1)} copy(bf16[256,2304]{1,0:T(8,128)(2,1)} %get-tuple-element.6) | data formatting | bytes 2359296
  58.4 0.0 copy-done
  58.4 0.7 %copy.11 = f32[288,256]{1,0:T(8,128)} copy(f32[288,256]{1,0:T(8,128)S(1)} %copy-done) | data formatting | bytes 589824
  59.2 0.0 copy-done.1
  59.2 0.6 %copy.12 = f32[2304]{0:T(1024)} copy(f32[2304]{0:T(1024)S(1)} %copy-done.1) | data formatting | bytes 18432
Async XLA Ops:
  56.0 2.4 %copy-start = (f32[288,256]{1,0:T(8,128)S(1)}, f32[288,256]{1,0:T(8,128)}, u32[]{:S(2)}) copy-start(f32[288,256]{1,0:T(8,128)} %get-tuple-element.7) | copy-start | bytes 884740
  56.0 3.1 %copy-start.1 = (f32[2304]{0:T(1024)S(1)}, f32[2304]{0:T(1024)}, u32[]{:S(2)}) copy-start(f32[2304]{0:T(1024)} %get-tuple-element.8) | copy-start | bytes 27652
where the time goes:
time: 59.9 us; the launch traced here: 59.8 us
  Pallas kernels  55.4 us (92%)
  local copies, waits for them, and re-layouts  3.72 us (6%)
  between operations  0.66 us (1%)
    pallas_call x1, Pallas kernels, fused(): pl.pallas_call(functools.partial(kernel, n_z, grad_scale), out_shape=(jax...  55.4 us
    unnamed x7, local copies, waits for them, and re-layouts  3.72 us

commit v1 on v0

--- a/solution.py
+++ b/solution.py
@@ -268,6 +268,17 @@
         copy.wait_send()
 
 
+def drain(tg_ref, wg_ref, gg_ref, tg_out, wg_out, gg_out, sem):
+    copies = [
+        pltpu.make_async_copy(src, dst, sem.at[n])
+        for n, (src, dst) in enumerate(((tg_ref, tg_out), (wg_ref, wg_out), (gg_ref, gg_out)))
+    ]
+    for copy in copies:
+        copy.start()
+    for copy in copies:
+        copy.wait()
+
+
 def fused(n_rep, n_grp, tokens, norm_gain, key_weight, key_grad):
     n_tok, features = tokens.shape
     rows, keys = key_weight.shape
@@ -283,7 +294,7 @@
             jax.ShapeDtypeStruct(block, f32),
             jax.ShapeDtypeStruct((features,), f32),
         ),
-        in_specs=[pl.BlockSpec(memory_space=pl.ANY)] * 4,
+        in_specs=[pl.BlockSpec(memory_space=pltpu.HBM)] * 4,
         out_specs=(vmem,) * 3,
         scratch_shapes=[
             pltpu.VMEM((n_tok, features), bf16),
@@ -309,10 +320,17 @@
             dma((2 * n_z + 2,)), dma((2 * n_z + 2,)),
         ],
         compiler_params=pltpu.CompilerParams(
-            collective_id=0, has_side_effects=True, vmem_limit_bytes=60 * 1024 * 1024
+            collective_id=0, has_side_effects=True, vmem_limit_bytes=40 * 1024 * 1024
         ),
-    )(tokens, norm_gain, key_weight, key_grad)
-    return token_grad, weight_grad, gain_grad
+    )(*(pltpu.with_memory_space_constraint(a, pltpu.MemorySpace.HBM) for a in (tokens, norm_gain, key_weight, key_grad)))
+    return pl.pallas_call(
+        drain,
+        out_shape=tuple(jax.ShapeDtypeStruct(a.shape, a.dtype) for a in (token_grad, weight_grad, gain_grad)),
+        in_specs=[vmem] * 3,
+        out_specs=(pl.BlockSpec(memory_space=pl.ANY),) * 3,
+        scratch_shapes=[dma((3,))],
+        compiler_params=pltpu.CompilerParams(vmem_limit_bytes=8 * 1024 * 1024),
+    )(token_grad, weight_grad, gain_grad)
 
 
 def plain(tokens, norm_gain, key_weight, key_grad):

time: 59.9 us -> 56.2 us (0.938)
  local copies, waits for them, and re-layouts: 3.72 us -> 0 us
    unnamed x7 -> x0, local copies, waits for them, and re-layouts: 3.72 us -> none
    pallas_call x0 -> x1, Pallas kernels: none -> 1.13 us  [fused(): pl.pallas_call(drain, out_shape=tuple((jax.ShapeDtypeStruct(a.shape, a.dt...]
    pallas_call x1, Pallas kernels: 55.4 us -> 54.2 us  [fused(): pl.pallas_call(functools.partial(kernel, n_z, grad_scale), out_shape=(jax...]
where the time goes in v1:
time: 56.2 us; the launch traced here: 56 us
  Pallas kernels  55.4 us (99%)
  between operations  0.64 us (1%)
    pallas_call x1, Pallas kernels, fused(): pl.pallas_call(functools.partial(kernel, n_z, grad_scale), out_shape=(jax...  54.2 us
    pallas_call x1, Pallas kernels, fused(): pl.pallas_call(drain, out_shape=tuple((jax.ShapeDtypeStruct(a.shape, a.dt...  1.13 us

profile of v1, /device:TPU:0, one launch (start us, length us, event | category | flops | bytes accessed | tf_op | source)
XLA Modules:
  0.0 56.0 jit_solution(6343359815576480926)
XLA Ops:
  0.6 54.2 %shard_map.67 = (bf16[256,2304]{1,0:T(8,128)(2,1)S(1)}, f32[288,256]{1,0:T(8,128)S(1)}, f32[2304]{0:T(1024)S(1)}) custom-call(bf16[256,2304]{1,0:T(8,128)(2,1)} %tok_hbm.1, f32[2304]{0:T(1024)} %gain_hbm.1, bf16[288,1024]{1,0:T(8,128)(2,1)} %w_ref.1, bf16[256,1024]{1,0:T(8,128)(2,1)} %kg_hbm.1), custom_call_target="tpu_custom_call" | custom-call | tf_op jit(solution)/shard_map/pallas_call | solution.py:290
  54.9 1.1 %shard_map.68 = (bf16[256,2304]{1,0:T(8,128)(2,1)}, f32[288,256]{1,0:T(8,128)}, f32[2304]{0:T(1024)}) custom-call(bf16[256,2304]{1,0:T(8,128)(2,1)S(1)} %get-tuple-element.6.tg_ref, f32[288,256]{1,0:T(8,128)S(1)} %get-tuple-element.7.wg_ref, f32[2304]{0:T(1024)S(1)} %get-tuple-element.8.gg_ref), custom_call_target="tpu_custom_call" | custom-call | tf_op jit(solution)/shard_map/pallas_call | solution.py:326

commit v2 on v1

v2 whole, which is shorter than its diff:
```python
import functools

import jax
import jax.numpy as jnp
from jax import lax
from jax.experimental import pallas as pl
from jax.experimental.pallas import tpu as pltpu
from jax.sharding import PartitionSpec as P

epsilon = 1e-06
MESH = pl.DeviceIdType.MESH
LANES = 128


def flip(i, bits):
    bit = 1
    while bit <= bits:
        if bits & bit:
            i = i + bit * (1 - 2 * lax.rem(lax.div(i, bit), 2))
        bit *= 2
    return i


HA, HR = 2, 2
PIECE, HOP, LEAD, AHEAD = 3.16, 1.9, 0.8, 10.0
PART_ORDER = [(3, 0), (2, 0), (3, 1), (2, 1), (0, 0), (1, 0), (0, 1), (1, 1)]


def messages():
    out = []

    def add(role, link, what, dst, arrives, needs, size):
        out.append(dict(role=role, link=link, what=what, dst=dst, arrives=arrives, needs=needs, size=size))

    for h in range(HA):
        size = PIECE / HA
        for role, me in (("E", 0), ("I", 1)):
            for q in (0, 1):
                for k in range(4):
                    needs = ("own",) if k == me else ("W", q, k, 0, h)
                    if q == 0:
                        add(role, "y", ("W", q, k, 0, h), role, ("W", q, k, 1, h), [needs], size)
                        add(role, "x", ("W", q, k, 1, h), role, ("W", 1, k, 1, h), [("W", 0, k, 1, h)], size)
                    if role == "E" and k == 0:
                        add(role, "z", ("W", q, k, 0, h), "I", ("W", q, 0, 0, h), [needs], size)
                    if role == "I" and k >= 1:
                        add(role, "z", ("W", q, k, 0, h), "E", ("W", q, k, 0, h), [needs], size)
                    if role == "I" and k <= 1:
                        add(role, "across", ("W", q, k, 0, h), "I", ("W", q, 3 - k, 0, h), [needs], size)
    for h in range(HR):
        size = PIECE / HR
        for s in (0, 1):
            for role in "EI":
                for k in range(4):
                    link = "x" if k in (0, 3) else "y"
                    add(role, link, ("one", k, s, h), role, ("in1", k, s, h), [("part", k, s, 1)], size)
            for k in (1, 2, 3):
                needs = [("part", k, s, 0), ("in1", k, s, h)]
                add("E", "z", ("sum", k, s, h), "I", ("inz", k, s, h), needs, size)
                if k > 1:
                    needs = needs + [("inz", k, s, h)]
                    add("I", "across", ("sum", k, s, h), "I", ("inx", 3 - k, s, h), needs, size)
            needs = [("part", 0, s, 0), ("in1", 0, s, h), ("inx", 0, s, h)]
            add("I", "z", ("sum", 0, s, h), "E", ("inz", 0, s, h), needs, size)
        needs = [("part", 0, 1, 0), ("in1", 0, 1, h), ("inz", 0, 1, h)]
        add("E", "y", ("sum", 0, 1, h), "E", ("fin", h), needs, size)
        needs = [("part", 1, 1, 0), ("in1", 1, 1, h), ("inz", 1, 1, h), ("inx", 1, 1, h)]
        add("I", "x", ("sum", 1, 1, h), "I", ("fin", h), needs, size)
    return out


def plan():
    copies = messages()
    known, users, tails = {}, {}, {}
    for role in "EI":
        known[role, ("own",)] = 0.9
        for i, (k, s) in enumerate(PART_ORDER):
            known[role, ("part", k, s, 1)] = 3.2 + 0.12 * i
            known[role, ("part", k, s, 0)] = 3.2 + 0.12 * (8 + i)
    for i, copy in enumerate(copies):
        for need in copy["needs"]:
            users.setdefault((copy["role"], need), []).append(i)

    def tail(i):
        if i not in tails:
            copy = copies[i]
            rest = AHEAD if copy["arrives"][0] == "W" else 1.5
            for j in users.get((copy["dst"], copy["arrives"]), []):
                rest = max(rest, tail(j))
            tails[i] = rest + copy["size"] + HOP
        return tails[i]

    free, left = {}, list(range(len(copies)))
    while left:
        best = None
        for i in left:
            copy = copies[i]
            needs = [(copy["role"], need) for need in copy["needs"]]
            if all(need in known for need in needs):
                link = free.get((copy["role"], copy["link"]), 0.0)
                ready = max(known[need] for need in needs)
                key = (round(max(link, ready), 3), -tail(i), i)
                if best is None or key < best[0]:
                    best = (key, i, ready)
        (start, _, _), i, ready = best
        copy = copies[i]
        left.remove(i)
        copy["start"], copy["ready"] = start, ready
        free[copy["role"], copy["link"]] = start + copy["size"]
        known[copy["dst"], copy["arrives"]] = start + copy["size"] + HOP
    steps = {}
    for role in "EI":
        todo = [(1.0, 0, ("norm",))]
        for k, s in PART_ORDER:
            for o in (1, 0):
                todo.append((known[role, ("part", k, s, o)], 1, ("part", k, s, o)))
        got = [(t, what) for (r, what), t in known.items() if r == role and what[0] == "W"]
        for t, what in got:
            todo.append((t, 2, what))
        near = max(t for t, what in got if what[2] < 2) + 1.4
        far = max(max(t for t, what in got) + 1.4, near + 1.8)
        for j in range(3):
            todo.append((near + 0.55 * j, 3, ("dot", 0, j)))
            todo.append((far + 0.55 * j, 3, ("dot", 1, j)))
        todo.append((far + 1.6, 3, ("gain", 1)))
        todo.append((far + 3.8, 3, ("gain", 2)))
        for j in range(3):
            todo.append((far + 1.7 + 0.2 * j, 4, ("grad", j)))
        for i, copy in enumerate(copies):
            if copy["role"] == role:
                todo.append((max(copy["ready"], copy["start"] - LEAD), 5 + i, ("send", copy)))
        steps[role] = [step for _, _, step in sorted(todo, key=lambda a: a[:2])]
    return steps


def kernel(
    n_z, grad_scale,
    tok_hbm, gain_hbm, w_hbm, kg_hbm,
    tg_ref, wg_ref, gg_ref,
    tok_ref, gain_ref, kg_ref, load_sem, wfull, normed, kgq, inv_ref, inner, dn, part, in1, inz, inx, fin, gsend, grecv, gain_row,
    send_sem, w_recv, c_recv, in1_recv, inz_recv, inx_recv, fin_recv, n_recv, k_recv, g_recv,
):
    rep, grp = lax.axis_index("rep"), lax.axis_index("grp")
    x, c = lax.div(rep, 2), lax.rem(rep, 2)
    z, y = lax.div(grp, 2), lax.rem(grp, 2)
    upper = lax.div(z, 2)
    n_tok, features = tok_ref.shape
    rows, cols = fin.shape
    peer_c = (2 * x + 1 - c, grp)
    peer_x = (2 * (1 - x) + c, grp)
    peer_cx = (2 * (1 - x) + 1 - c, grp)
    peer_y = (rep, 2 * z + 1 - y)
    peer_z = [None] + [(rep, 2 * flip(z, k) + y) for k in range(1, n_z)]
    group = [peer_y]
    for k in range(1, n_z):
        group += [peer_z[k], (rep, 2 * flip(z, k) + 1 - y)]
    bf16, f32 = jnp.bfloat16, jnp.float32

    def row_at(k, yy, h=0, parts=1):
        g = 2 * (k + upper * (3 - 2 * k)) + (1 - y if yy else y)
        return pl.ds(pl.multiple_of(g * rows + h * (rows // parts), 16), rows // parts)

    def col_at(xx):
        r = 2 * (1 - x if xx else x) + c
        return pl.ds(pl.multiple_of(r * cols, LANES), cols)

    own_rows = pl.ds(pl.multiple_of(grp * rows, 16), rows)
    loads = [
        pltpu.make_async_copy(src, dst, load_sem.at[n])
        for n, (src, dst) in enumerate(
            ((w_hbm, wfull.at[own_rows, :]), (tok_hbm, tok_ref), (kg_hbm, kg_ref), (gain_hbm, gain_ref))
        )
    ]
    for load in loads:
        load.start()

    barrier = pltpu.get_barrier_semaphore()
    peers = [peer_c, peer_x, peer_cx] + group
    for peer in peers:
        pl.semaphore_signal(barrier, inc=1, device_id=peer, device_id_type=MESH)
    pl.semaphore_wait(barrier, len(peers))
    loads[0].wait()

    def role(name, steps):
        sends = []

        def send(src, dst, r_sem, peer):
            copy = pltpu.make_async_remote_copy(
                src_ref=src, dst_ref=dst, send_sem=send_sem.at[len(sends)], recv_sem=r_sem,
                device_id=peer, device_id_type=MESH,
            )
            copy.start()
            sends.append(copy)

        waited = set()

        def arrived(dst, sem, key):
            if key not in waited:
                waited.add(key)
                pltpu.make_async_remote_copy(
                    src_ref=dst, dst_ref=dst, send_sem=sem, recv_sem=sem, device_id=peer_c, device_id_type=MESH
                ).wait_recv()

        def split(h):
            return pl.ds(h * (rows // HR), rows // HR)

        def w_piece(q, k, yy, h):
            return wfull.at[row_at(k, yy, h, HA), col_at(q)]

        def got(what):
            kind = what[0]
            if kind == "W":
                _, q, k, yy, h = what
                arrived(w_piece(q, k, yy, h), w_recv.at[q, k, yy, h], what)
            elif kind == "fin":
                arrived(fin.at[split(what[1]), :], fin_recv.at[what[1]], what)
            elif kind in ("in1", "inz", "inx"):
                _, k, s, h = what
                buf, sem = {"in1": (in1, in1_recv), "inz": (inz, inz_recv), "inx": (inx, inx_recv)}[kind]
                arrived(buf.at[k, s, split(h), :], sem.at[k, s, h], what)

        def summed(k, s, h):
            at = split(h)
            total = part[k, s, 0, at, :].astype(f32)
            terms = [("in1", in1)]
            if name == "E":
                terms += [("inz", inz)] if k == 0 else []
            else:
                terms += ([("inz", inz)] if k > 0 else []) + ([("inx", inx)] if k < 2 else [])
            for kind, buf in terms:
                got((kind, k, s, h))
                total = total + buf[k, s, at, :].astype(f32)
            return total

        def send_copy(copy):
            what, arrives, link = copy["what"], copy["arrives"], copy["link"]
            peer = {"x": peer_x, "y": peer_y, "z": peer_z[1], "across": peer_z[3]}[link]
            for need in copy["needs"]:
                got(need)
            if what[0] == "W":
                _, q, k, yy, h = what
                piece = w_piece(q, k, yy, h)
                send(piece, piece, w_recv.at[arrives[1:]], peer)
                return
            if arrives[0] == "fin":
                dst, sem = fin.at[split(arrives[1]), :], fin_recv.at[arrives[1]]
            else:
                _, k, s, h = arrives
                buf, sems = {"in1": (in1, in1_recv), "inz": (inz, inz_recv), "inx": (inx, inx_recv)}[arrives[0]]
                dst, sem = buf.at[k, s, split(h), :], sems.at[k, s, h]
            _, k, s, h = what
            if what[0] == "one":
                send(part.at[k, s, 1, split(h), :], dst, sem, peer)
            else:
                part[k, s, 0, split(h), :] = summed(k, s, h).astype(bf16)
                send(part.at[k, s, 0, split(h), :], dst, sem, peer)

        def norm():
            loads[1].wait()
            acc = None
            for j in range(features // LANES):
                t = tok_ref[:, j * LANES:(j + 1) * LANES].astype(f32)
                acc = t * t if acc is None else acc + t * t
            inv = lax.rsqrt(jnp.sum(acc, axis=1, keepdims=True) / features + epsilon)
            inv_ref[...] = inv
            inner[...] = jnp.zeros_like(inner)
            loads[3].wait()
            for j in range(features // LANES):
                at = slice(j * LANES, (j + 1) * LANES)
                t = tok_ref[:, at].astype(f32)
                normed[at, :n_tok] = (t * inv * gain_ref[at].reshape(1, -1)).T.astype(bf16)
            loads[2].wait()
            for xx in (0, 1):
                kgq[xx, :n_tok, :] = kg_ref[:, col_at(xx)]
                theirs = pl.ds(pl.multiple_of((2 * (1 - x if xx else x) + 1 - c) * cols, LANES), cols)
                send(kg_ref.at[:, theirs], kgq.at[xx, pl.ds(n_tok, n_tok), :], k_recv.at[xx], peer_c)
            for k, yy in ((3, 0), (2, 1), (3, 1), (0, 0), (1, 1), (0, 1), (2, 0), (1, 0)):
                send(
                    normed.at[row_at(k, yy), pl.ds(0, n_tok)], normed.at[row_at(k, yy), pl.ds(n_tok, n_tok)],
                    n_recv.at[k, yy], peer_c,
                )

        def block(k, s, o):
            yy, xx = (s, o) if k in (0, 3) else (o, s)
            arrived(kgq.at[xx, pl.ds(n_tok, n_tok), :], k_recv.at[xx], ("kg", xx))
            arrived(normed.at[row_at(k, yy), pl.ds(n_tok, n_tok)], n_recv.at[k, yy], ("normed", k, yy))
            part[k, s, o] = jnp.dot(
                normed[row_at(k, yy), :], kgq[xx], preferred_element_type=f32
            ).astype(bf16)

        me = 0 if name == "E" else 1

        def dots(far, j):
            if j == 0:
                for k in (2, 3) if far else (0, 1):
                    for yy in (0, 1):
                        if (k, yy) != (me, 0):
                            for q in (0, 1):
                                for h in range(HA):
                                    got(("W", q, k, yy, h))
                                    at = (row_at(k, yy, h, HA), other_col(q))
                                    arrived(wfull.at[at], c_recv.at[q, k, yy, h], ("C", q, k, yy, h))
            wide = features // 6
            base = (1 - upper if far else upper) * (features // 2) + j * wide
            at = pl.ds(pl.multiple_of(base, LANES), wide)
            d = lax.dot_general(
                kg_ref[...], wfull[at, :], (((1,), (1,)), ((), ())), preferred_element_type=f32
            )
            dn[:, at] = d
            dt = d * tok_ref[:, at].astype(f32)
            gsend[0, :, at] = jnp.sum(dt * inv_ref[...], axis=0, keepdims=True)
            gain_at = gain_row[:, at]
            scaled = dt * gain_at
            add = scaled[:, :LANES]
            for n in range(1, wide // LANES):
                add = add + scaled[:, n * LANES:(n + 1) * LANES]
            inner[...] = inner[...] + add

        def other_col(q):
            r = 2 * (1 - x if q else x) + 1 - c
            return pl.ds(pl.multiple_of(r * cols, LANES), cols)

        def gain(stage):
            if stage == 1:
                for n, peer in enumerate((peer_c, peer_x, peer_cx)):
                    send(gsend.at[0], grecv.at[n], g_recv.at[n], peer)
                return
            for n in range(3):
                arrived(grecv.at[n], g_recv.at[n], ("g", n))
            gsend[1] = (gsend[0] + grecv[0]) + (grecv[1] + grecv[2])
            for n, peer in enumerate(group):
                send(gsend.at[1], grecv.at[3 + n], g_recv.at[3 + n], peer)

        def grad(j):
            inv = inv_ref[...]
            pull = inv * inv * (jnp.sum(inner[...], axis=1, keepdims=True) / features)
            wide = features // 9
            for n in range(3 * j, 3 * j + 3):
                at = slice(n * wide, (n + 1) * wide)
                t = tok_ref[:, at].astype(f32)
                tg_ref[:, at] = (inv * (dn[:, at] * gain_ref[at].reshape(1, -1) - t * pull)).astype(bf16)

        for step in steps:
            kind = step[0]
            if kind == "send":
                send_copy(step[1])
            elif kind == "norm":
                norm()
                for j in range(features // LANES):
                    at = slice(j * LANES, (j + 1) * LANES)
                    gain_row[:, at] = gain_ref[at].reshape(1, -1)
            elif kind == "part":
                block(*step[1:])
            elif kind == "W":
                _, q, k, yy, h = step
                got(step)
                piece = w_piece(q, k, yy, h)
                send(piece, piece, c_recv.at[q, k, yy, h], peer_c)
            elif kind == "dot":
                dots(*step[1:])
            elif kind == "gain":
                gain(step[1])
            else:
                grad(step[1])

        for h in range(HR):
            total = summed(me, 0, h)
            got(("fin", h))
            wg_ref[split(h), :] = (total + fin[split(h), :].astype(f32)) * grad_scale
        terms = [gsend[1]]
        for n in range(3, 3 + len(group)):
            arrived(grecv.at[n], g_recv.at[n], ("g", n))
            terms.append(grecv[n])
        while len(terms) > 1:
            terms = [terms[i] + terms[i + 1] for i in range(0, len(terms), 2)]
        total = terms[0] * grad_scale
        for j in range(features // LANES):
            at = slice(j * LANES, (j + 1) * LANES)
            gg_ref[at] = total[:, at].reshape(LANES)
        for copy in sends:
            copy.wait_send()

    steps = plan()
    end = lax.rem(lax.div(z + 1, 2), 2) == 0
    for name, here in (("E", end), ("I", jnp.logical_not(end))):
        pl.when(here)(functools.partial(role, name, steps[name]))


def drain(tg_ref, wg_ref, gg_ref, tg_out, wg_out, gg_out, sem):
    copies = [
        pltpu.make_async_copy(src, dst, sem.at[n])
        for n, (src, dst) in enumerate(((tg_ref, tg_out), (wg_ref, wg_out), (gg_ref, gg_out)))
    ]
    for copy in copies:
        copy.start()
    for copy in copies:
        copy.wait()


def fused(n_rep, n_grp, tokens, norm_gain, key_weight, key_grad):
    n_tok, features = tokens.shape
    rows, keys = key_weight.shape
    cols, n_z = keys // n_rep, n_grp // 2
    grad_scale = (n_tok * n_rep * n_grp) ** (-0.5)
    vmem = pl.BlockSpec(memory_space=pltpu.VMEM)
    bf16, f32, dma = jnp.bfloat16, jnp.float32, pltpu.SemaphoreType.DMA
    block = (rows, cols)
    token_grad, weight_grad, gain_grad = pl.pallas_call(
        functools.partial(kernel, n_z, grad_scale),
        out_shape=(
            jax.ShapeDtypeStruct((n_tok, features), bf16),
            jax.ShapeDtypeStruct(block, f32),
            jax.ShapeDtypeStruct((features,), f32),
        ),
        in_specs=[pl.BlockSpec(memory_space=pltpu.HBM)] * 4,
        out_specs=(vmem,) * 3,
        scratch_shapes=[
            pltpu.VMEM((n_tok, features), bf16),
            pltpu.VMEM((features,), f32),
            pltpu.VMEM((n_tok, keys), bf16),
            dma((4,)),
            pltpu.VMEM((features, keys), bf16),
            pltpu.VMEM((features, 2 * n_tok), bf16),
            pltpu.VMEM((2, 2 * n_tok, cols), bf16),
            pltpu.VMEM((n_tok, 1), f32),
            pltpu.VMEM((n_tok, LANES), f32),
            pltpu.VMEM((n_tok, features), f32),
            pltpu.VMEM((n_z, 2, 2) + block, bf16),
            pltpu.VMEM((n_z, 2) + block, bf16),
            pltpu.VMEM((n_z, 2) + block, bf16),
            pltpu.VMEM((2, 2) + block, bf16),
            pltpu.VMEM(block, bf16),
            pltpu.VMEM((2, 1, features), f32),
            pltpu.VMEM((2 * n_z + 2, 1, features), f32),
            pltpu.VMEM((1, features), f32),
            dma((160,)),
            dma((2, n_z, 2, HA)), dma((2, n_z, 2, HA)),
            dma((n_z, 2, HR)), dma((n_z, 2, HR)), dma((2, 2, HR)), dma((HR,)),
            dma((n_z, 2)), dma((2,)), dma((2 * n_z + 2,)),
        ],
        compiler_params=pltpu.CompilerParams(
            collective_id=0, has_side_effects=True, vmem_limit_bytes=40 * 1024 * 1024
        ),
    )(*(pltpu.with_memory_space_constraint(a, pltpu.MemorySpace.HBM) for a in (tokens, norm_gain, key_weight, key_grad)))
    return pl.pallas_call(
        drain,
        out_shape=tuple(jax.ShapeDtypeStruct(a.shape, a.dtype) for a in (token_grad, weight_grad, gain_grad)),
        in_specs=[vmem] * 3,
        out_specs=(pl.BlockSpec(memory_space=pl.ANY),) * 3,
        scratch_shapes=[dma((3,))],
        compiler_params=pltpu.CompilerParams(vmem_limit_bytes=8 * 1024 * 1024),
    )(token_grad, weight_grad, gain_grad)


def plain(tokens, norm_gain, key_weight, key_grad):
    total_tokens = tokens.shape[0] * lax.axis_size("rep") * lax.axis_size("grp")
    grad_scale = total_tokens ** (-0.5)
    wide_tokens = tokens.astype(jnp.float32)
    inv_rms = lax.rsqrt(jnp.mean(wide_tokens * wide_tokens, axis=1, keepdims=True) + epsilon)
    normed = (wide_tokens * inv_rms * norm_gain).astype(jnp.bfloat16)
    partial_value = lax.dot_general(
        normed, key_grad, (((0,), (0,)), ((), ())), preferred_element_type=jnp.float32
    )
    d_normed = lax.dot_general(
        key_grad,
        lax.all_gather(key_weight, "grp", axis=0, tiled=True),
        (((1,), (1,)), ((), ())),
        preferred_element_type=jnp.float32,
    )
    section_one = lax.psum_scatter(
        partial_value.astype(jnp.bfloat16), "rep", scatter_dimension=1, tiled=True
    ).astype(jnp.float32)
    weight_sum = lax.psum_scatter(section_one, "grp", scatter_dimension=0, tiled=True)
    gain_local = jnp.sum(d_normed * wide_tokens * inv_rms, axis=0)
    gain_total = lax.psum(gain_local, ("rep", "grp"))
    scaled = d_normed * norm_gain
    inner_mean = jnp.mean(scaled * wide_tokens, axis=1, keepdims=True)
    token_grad = (inv_rms * (scaled - wide_tokens * inv_rms * inv_rms * inner_mean)).astype(
        jnp.bfloat16
    )
    return (token_grad, weight_sum * grad_scale, gain_total * grad_scale)


def shards(tokens, norm_gain, key_weight, key_grad):
    n_rep, n_grp = lax.axis_size("rep"), lax.axis_size("grp")
    n_z = n_grp // 2
    if (
        n_rep == 2 * 2 and n_grp == 2 * 4
        and key_weight.shape[1] % (n_rep * LANES) == 0 and key_weight.shape[0] % 32 == 0
        and tokens.shape[1] % (18 * LANES) == 0 and tokens.shape[0] % LANES == 0
    ):
        return fused(n_rep, n_grp, tokens, norm_gain, key_weight, key_grad)
    return plain(tokens, norm_gain, key_weight, key_grad)


def solution(mesh):
    in_specs = (P(("rep", "grp"), None), P(), P("grp", None), P(("rep", "grp"), None))
    out_specs = (P(("rep", "grp"), None), P("grp", "rep"), P())
    return jax.shard_map(shards, mesh=mesh, in_specs=in_specs, out_specs=out_specs, check_vma=False)
```

time: 56.2 us -> 47 us (0.84)
  Pallas kernels: 55.4 us -> 46.1 us
    pallas_call x1, Pallas kernels: 54.2 us -> 44.9 us  [fused(): pl.pallas_call(functools.partial(kernel, n_z, grad_scale), out_shape=(jax...]
where the time goes in v2:
time: 47 us; the launch traced here: 46.9 us
  Pallas kernels  46.1 us (98%)
  between operations  0.8 us (2%)
    pallas_call x1, Pallas kernels, fused(): pl.pallas_call(functools.partial(kernel, n_z, grad_scale), out_shape=(jax...  44.9 us
    pallas_call x1, Pallas kernels, fused(): pl.pallas_call(drain, out_shape=tuple((jax.ShapeDtypeStruct(a.shape, a.dt...  1.13 us

profile of v2, /device:TPU:0, one launch (start us, length us, event | category | flops | bytes accessed | tf_op | source)
XLA Modules:
  0.0 46.9 jit_solution(8863988336702895558)
XLA Ops:
  0.6 44.9 %shard_map.67 = (bf16[256,2304]{1,0:T(8,128)(2,1)S(1)}, f32[288,256]{1,0:T(8,128)S(1)}, f32[2304]{0:T(1024)S(1)}) custom-call(bf16[256,2304]{1,0:T(8,128)(2,1)} %tok_hbm.1, f32[2304]{0:T(1024)} %gain_hbm.1, bf16[288,1024]{1,0:T(8,128)(2,1)} %w_hbm.1, bf16[256,1024]{1,0:T(8,128)(2,1)} %kg_hbm.1), custom_call_target="tpu_custom_call" | custom-call | tf_op jit(solution)/shard_map/pallas_call | solution.py:408
  45.6 1.1 %shard_map.68 = (bf16[256,2304]{1,0:T(8,128)(2,1)}, f32[288,256]{1,0:T(8,128)}, f32[2304]{0:T(1024)}) custom-call(bf16[256,2304]{1,0:T(8,128)(2,1)S(1)} %get-tuple-element.6.tg_ref, f32[288,256]{1,0:T(8,128)S(1)} %get-tuple-element.7.wg_ref, f32[2304]{0:T(1024)S(1)} %get-tuple-element.8.gg_ref), custom_call_target="tpu_custom_call" | custom-call | tf_op jit(solution)/shard_map/pallas_call | solution.py:445

commit v3 on v2

--- a/solution.py
+++ b/solution.py
@@ -21,9 +21,11 @@
     return i
 
 
-HA, HR = 2, 2
-PIECE, HOP, LEAD, AHEAD = 3.16, 1.9, 0.8, 10.0
-PART_ORDER = [(3, 0), (2, 0), (3, 1), (2, 1), (0, 0), (1, 0), (0, 1), (1, 1)]
+HA, HR = 2, 3
+PIECE, HOP, LEAD, AHEAD = 3.2, 2.5, 1.2, 11.0
+OWN, PART, STEP, GUARD = 0.4, 2.7, 0.45, 1.0
+XF = {(0, 0), (1, 0), (1, 1), (2, 0), (2, 1), (3, 0)}
+PART_ORDER = [(3, 1), (2, 1), (2, 0), (3, 0), (0, 1), (1, 1), (1, 0), (0, 0)]
 
 
 def messages():
@@ -52,20 +54,21 @@
         for s in (0, 1):
             for role in "EI":
                 for k in range(4):
-                    link = "x" if k in (0, 3) else "y"
-                    add(role, link, ("one", k, s, h), role, ("in1", k, s, h), [("part", k, s, 1)], size)
+                    first = (k, h) in XF
+                    link, needs = ("x", ("part", k, 1)) if first else ("y", ("part", k, s))
+                    add(role, link, ("one", k, s, h), role, ("in1", k, s, h), [needs], size)
+            kept = [("part", k, 0 if (k, h) in XF else s) for k in range(4)]
             for k in (1, 2, 3):
-                needs = [("part", k, s, 0), ("in1", k, s, h)]
+                needs = [kept[k], ("in1", k, s, h)]
                 add("E", "z", ("sum", k, s, h), "I", ("inz", k, s, h), needs, size)
                 if k > 1:
                     needs = needs + [("inz", k, s, h)]
                     add("I", "across", ("sum", k, s, h), "I", ("inx", 3 - k, s, h), needs, size)
-            needs = [("part", 0, s, 0), ("in1", 0, s, h), ("inx", 0, s, h)]
+            needs = [kept[0], ("in1", 0, s, h), ("inx", 0, s, h)]
             add("I", "z", ("sum", 0, s, h), "E", ("inz", 0, s, h), needs, size)
-        needs = [("part", 0, 1, 0), ("in1", 0, 1, h), ("inz", 0, 1, h)]
-        add("E", "y", ("sum", 0, 1, h), "E", ("fin", h), needs, size)
-        needs = [("part", 1, 1, 0), ("in1", 1, 1, h), ("inz", 1, 1, h), ("inx", 1, 1, h)]
-        add("I", "x", ("sum", 1, 1, h), "I", ("fin", h), needs, size)
+        for role, k in (("E", 0), ("I", 1)):
+            needs = [kept[k], ("in1", k, 1, h), ("inz", k, 1, h)] + ([("inx", 1, 1, h)] if k else [])
+            add(role, "y" if (k, h) in XF else "x", ("sum", k, 1, h), role, ("fin", h), needs, size)
     return out
 
 
@@ -73,10 +76,9 @@
     copies = messages()
     known, users, tails = {}, {}, {}
     for role in "EI":
-        known[role, ("own",)] = 0.9
-        for i, (k, s) in enumerate(PART_ORDER):
-            known[role, ("part", k, s, 1)] = 3.2 + 0.12 * i
-            known[role, ("part", k, s, 0)] = 3.2 + 0.12 * (8 + i)
+        known[role, ("own",)] = OWN
+        for i, (k, xx) in enumerate(PART_ORDER):
+            known[role, ("part", k, xx)] = PART + STEP * i
     for i, copy in enumerate(copies):
         for need in copy["needs"]:
             users.setdefault((copy["role"], need), []).append(i)
@@ -90,45 +92,66 @@
             tails[i] = rest + copy["size"] + HOP
         return tails[i]
 
-    free, left = {}, list(range(len(copies)))
-    while left:
-        best = None
-        for i in left:
+    def schedule(known, blocked):
+        free, left = {}, list(range(len(copies)))
+        while left:
+            best = None
+            for i in left:
+                copy = copies[i]
+                needs = [(copy["role"], need) for need in copy["needs"]]
+                if all(need in known for need in needs):
+                    ready = max(known[need] for need in needs)
+                    start = max(free.get((copy["role"], copy["link"]), 0.0), ready)
+                    low, high = blocked.get((copy["role"], copy["link"]), (0.0, 0.0))
+                    start = high if low < start < high else start
+                    key = (round(start, 3), -tail(i), i)
+                    if best is None or key < best[0]:
+                        best = (key, i, ready)
+            (start, _, _), i, ready = best
             copy = copies[i]
-            needs = [(copy["role"], need) for need in copy["needs"]]
-            if all(need in known for need in needs):
-                link = free.get((copy["role"], copy["link"]), 0.0)
-                ready = max(known[need] for need in needs)
-                key = (round(max(link, ready), 3), -tail(i), i)
-                if best is None or key < best[0]:
-                    best = (key, i, ready)
-        (start, _, _), i, ready = best
-        copy = copies[i]
-        left.remove(i)
-        copy["start"], copy["ready"] = start, ready
-        free[copy["role"], copy["link"]] = start + copy["size"]
-        known[copy["dst"], copy["arrives"]] = start + copy["size"] + HOP
+            left.remove(i)
+            copy["start"], copy["ready"] = start, ready
+            free[copy["role"], copy["link"]] = start + copy["size"]
+            known[copy["dst"], copy["arrives"]] = start + copy["size"] + HOP
+        return known
+
+    def marks(known, role):
+        got = [(t, what) for (r, what), t in known.items() if r == role and what[0] == "W"]
+        near = max(t for t, what in got if what[2] < 2) + 2.0
+        early = max(max(t for t, what in got if what[2] == 2) + 1.8, near + 1.5)
+        far = max(max(t for t, what in got) + 1.4, early + 0.5)
+        return got, near, early, far
+
+    first = schedule(dict(known), {})
+    blocked = {}
+    for role in "EI":
+        gain = marks(first, role)[3] + 1.1
+        blocked[role, "x"] = (gain - GUARD, gain + 0.1)
+    known = schedule(known, blocked)
     steps = {}
     for role in "EI":
-        todo = [(1.0, 0, ("norm",))]
-        for k, s in PART_ORDER:
-            for o in (1, 0):
-                todo.append((known[role, ("part", k, s, o)], 1, ("part", k, s, o)))
-        got = [(t, what) for (r, what), t in known.items() if r == role and what[0] == "W"]
+        todo = [(0.3, 0, ("norm",))]
+        for k, xx in PART_ORDER:
+            todo.append((known[role, ("part", k, xx)], 1, ("part", k, xx)))
+        got, near, early, far = marks(known, role)
         for t, what in got:
             todo.append((t, 2, what))
-        near = max(t for t, what in got if what[2] < 2) + 1.4
-        far = max(max(t for t, what in got) + 1.4, near + 1.8)
         for j in range(3):
             todo.append((near + 0.55 * j, 3, ("dot", 0, j)))
-            todo.append((far + 0.55 * j, 3, ("dot", 1, j)))
-        todo.append((far + 1.6, 3, ("gain", 1)))
-        todo.append((far + 3.8, 3, ("gain", 2)))
+            todo.append((far + 0.55 * (j - 1) if j else early, 3, ("dot", 1, j)))
+        gain = marks(first, role)[3] + 1.1
+        todo.append((gain, 3, ("gain", 1)))
+        last = max(copy["start"] for copy in copies if copy["role"] == role)
+        todo.append((max(far + 4.0, last - LEAD + 0.1), 3, ("gain", 2)))
         for j in range(3):
             todo.append((far + 1.7 + 0.2 * j, 4, ("grad", j)))
         for i, copy in enumerate(copies):
             if copy["role"] == role:
-                todo.append((max(copy["ready"], copy["start"] - LEAD), 5 + i, ("send", copy)))
+                t = copy["start"] - LEAD
+                if copy["link"] == "x" and copy["start"] > gain:
+                    t = max(t, gain + 0.01)
+                t = 0.0 if copy["needs"] == [("own",)] and t < 1.0 else t
+                todo.append((max(copy["ready"], t), 5 + i, ("send", copy)))
         steps[role] = [step for _, _, step in sorted(todo, key=lambda a: a[:2])]
     return steps
 
@@ -174,11 +197,18 @@
     for load in loads:
         load.start()
 
+    end = lax.rem(lax.div(z + 1, 2), 2) == 0
+    inside = jnp.logical_not(end)
     barrier = pltpu.get_barrier_semaphore()
-    peers = [peer_c, peer_x, peer_cx] + group
+    peers = [peer_c, peer_x, peer_y, peer_z[1]]
     for peer in peers:
         pl.semaphore_signal(barrier, inc=1, device_id=peer, device_id_type=MESH)
-    pl.semaphore_wait(barrier, len(peers))
+
+    @pl.when(inside)
+    def _():
+        pl.semaphore_signal(barrier, inc=1, device_id=peer_z[3], device_id_type=MESH)
+
+    pl.semaphore_wait(barrier, len(peers) + inside.astype(jnp.int32))
     loads[0].wait()
 
     def role(name, steps):
@@ -186,7 +216,7 @@
 
         def send(src, dst, r_sem, peer):
             copy = pltpu.make_async_remote_copy(
-                src_ref=src, dst_ref=dst, send_sem=send_sem.at[len(sends)], recv_sem=r_sem,
+                src_ref=src, dst_ref=dst, send_sem=send_sem, recv_sem=r_sem,
                 device_id=peer, device_id_type=MESH,
             )
             copy.start()
@@ -217,11 +247,18 @@
             elif kind in ("in1", "inz", "inx"):
                 _, k, s, h = what
                 buf, sem = {"in1": (in1, in1_recv), "inz": (inz, inz_recv), "inx": (inx, inx_recv)}[kind]
+                k = k - 1 if kind == "inz" and k else k
                 arrived(buf.at[k, s, split(h), :], sem.at[k, s, h], what)
+
+        def kept(k, s, h):
+            return (k, s, 0, split(h), slice(None)) if (k, h) in XF else (k, 0, s, split(h), slice(None))
+
+        def given(k, s, h):
+            return (k, s, 1, split(h), slice(None)) if (k, h) in XF else (k, 1, s, split(h), slice(None))
 
         def summed(k, s, h):
             at = split(h)
-            total = part[k, s, 0, at, :].astype(f32)
+            total = part[kept(k, s, h)].astype(f32)
             terms = [("in1", in1)]
             if name == "E":
                 terms += [("inz", inz)] if k == 0 else []
@@ -229,7 +266,8 @@
                 terms += ([("inz", inz)] if k > 0 else []) + ([("inx", inx)] if k < 2 else [])
             for kind, buf in terms:
                 got((kind, k, s, h))
-                total = total + buf[k, s, at, :].astype(f32)
+                slot = k - 1 if kind == "inz" and k else k
+                total = total + buf[slot, s, at, :].astype(f32)
             return total
 
         def send_copy(copy):
@@ -247,15 +285,20 @@
             else:
                 _, k, s, h = arrives
                 buf, sems = {"in1": (in1, in1_recv), "inz": (inz, inz_recv), "inx": (inx, inx_recv)}[arrives[0]]
+                k = k - 1 if arrives[0] == "inz" and k else k
                 dst, sem = buf.at[k, s, split(h), :], sems.at[k, s, h]
             _, k, s, h = what
             if what[0] == "one":
-                send(part.at[k, s, 1, split(h), :], dst, sem, peer)
+                send(part.at[given(k, s, h)], dst, sem, peer)
             else:
-                part[k, s, 0, split(h), :] = summed(k, s, h).astype(bf16)
-                send(part.at[k, s, 0, split(h), :], dst, sem, peer)
+                part[kept(k, s, h)] = summed(k, s, h).astype(bf16)
+                send(part.at[kept(k, s, h)], dst, sem, peer)
 
         def norm():
+            loads[2].wait()
+            for xx in (1, 0):
+                theirs = pl.ds(pl.multiple_of((2 * (1 - x if xx else x) + 1 - c) * cols, LANES), cols)
+                send(kg_ref.at[:, theirs], kgq.at[xx, pl.ds(n_tok, n_tok), :], k_recv, peer_c)
             loads[1].wait()
             acc = None
             for j in range(features // LANES):
@@ -267,41 +310,46 @@
             loads[3].wait()
             for j in range(features // LANES):
                 at = slice(j * LANES, (j + 1) * LANES)
-                t = tok_ref[:, at].astype(f32)
-                normed[at, :n_tok] = (t * inv * gain_ref[at].reshape(1, -1)).T.astype(bf16)
-            loads[2].wait()
+                gain_row[:, at] = gain_ref[at].reshape(1, -1)
+            half = features // 2
+            for far in (1, 0):
+                for j in range(half // LANES):
+                    base = (1 - upper if far else upper) * half + j * LANES
+                    at = pl.ds(pl.multiple_of(base, LANES), LANES)
+                    t = tok_ref[:, at].astype(f32)
+                    normed[at, :n_tok] = (t * inv * gain_row[:, at]).T.astype(bf16)
+                for k in (3, 2) if far else (0, 1):
+                    send(normed.at[pair_at(k), pl.ds(0, n_tok)], theirs_at(k), n_recv.at[k], peer_c)
             for xx in (0, 1):
                 kgq[xx, :n_tok, :] = kg_ref[:, col_at(xx)]
-                theirs = pl.ds(pl.multiple_of((2 * (1 - x if xx else x) + 1 - c) * cols, LANES), cols)
-                send(kg_ref.at[:, theirs], kgq.at[xx, pl.ds(n_tok, n_tok), :], k_recv.at[xx], peer_c)
-            for k, yy in ((3, 0), (2, 1), (3, 1), (0, 0), (1, 1), (0, 1), (2, 0), (1, 0)):
-                send(
-                    normed.at[row_at(k, yy), pl.ds(0, n_tok)], normed.at[row_at(k, yy), pl.ds(n_tok, n_tok)],
-                    n_recv.at[k, yy], peer_c,
-                )
-
-        def block(k, s, o):
-            yy, xx = (s, o) if k in (0, 3) else (o, s)
-            arrived(kgq.at[xx, pl.ds(n_tok, n_tok), :], k_recv.at[xx], ("kg", xx))
-            arrived(normed.at[row_at(k, yy), pl.ds(n_tok, n_tok)], n_recv.at[k, yy], ("normed", k, yy))
-            part[k, s, o] = jnp.dot(
-                normed[row_at(k, yy), :], kgq[xx], preferred_element_type=f32
-            ).astype(bf16)
+
+        def pair_at(k):
+            return pl.ds(pl.multiple_of(2 * rows * (k + upper * (3 - 2 * k)), 16), 2 * rows)
+
+        def theirs_at(k):
+            return normed.at[pair_at(k), pl.ds(n_tok, n_tok)]
+
+        def block(k, xx):
+            arrived(kgq.at[:, pl.ds(n_tok, n_tok), :], k_recv, "kg")
+            arrived(theirs_at(k), n_recv.at[k], ("normed", k))
+            both = jnp.dot(normed[pair_at(k), :], kgq[xx], preferred_element_type=f32).astype(bf16)
+            part[k, y, xx] = both[:rows]
+            part[k, 1 - y, xx] = both[rows:]
 
         me = 0 if name == "E" else 1
 
         def dots(far, j):
-            if j == 0:
-                for k in (2, 3) if far else (0, 1):
-                    for yy in (0, 1):
-                        if (k, yy) != (me, 0):
-                            for q in (0, 1):
-                                for h in range(HA):
-                                    got(("W", q, k, yy, h))
-                                    at = (row_at(k, yy, h, HA), other_col(q))
-                                    arrived(wfull.at[at], c_recv.at[q, k, yy, h], ("C", q, k, yy, h))
+            for k in ([0, 1] if j == 0 else []) if not far else [2 if j == 0 else 3]:
+                shards = [yy for yy in (0, 1) if (k, yy) != (me, 0)]
+                for yy in shards:
+                    for q in (0, 1):
+                        for h in range(HA):
+                            got(("W", q, k, yy, h))
+                amount = wfull.at[pl.ds(0, len(shards) * rows), pl.ds(0, 2 * cols)]
+                arrived(amount, c_recv.at[k], ("C", k))
             wide = features // 6
-            base = (1 - upper if far else upper) * (features // 2) + j * wide
+            side = 1 - upper if far else upper
+            base = side * (features // 2) + (j + upper * (2 - 2 * j)) * wide
             at = pl.ds(pl.multiple_of(base, LANES), wide)
             d = lax.dot_general(
                 kg_ref[...], wfull[at, :], (((1,), (1,)), ((), ())), preferred_element_type=f32
@@ -316,20 +364,15 @@
                 add = add + scaled[:, n * LANES:(n + 1) * LANES]
             inner[...] = inner[...] + add
 
-        def other_col(q):
-            r = 2 * (1 - x if q else x) + 1 - c
-            return pl.ds(pl.multiple_of(r * cols, LANES), cols)
-
         def gain(stage):
             if stage == 1:
                 for n, peer in enumerate((peer_c, peer_x, peer_cx)):
-                    send(gsend.at[0], grecv.at[n], g_recv.at[n], peer)
+                    send(gsend.at[0], grecv.at[n], g_recv.at[0], peer)
                 return
-            for n in range(3):
-                arrived(grecv.at[n], g_recv.at[n], ("g", n))
+            arrived(grecv.at[pl.ds(0, 3)], g_recv.at[0], "g0")
             gsend[1] = (gsend[0] + grecv[0]) + (grecv[1] + grecv[2])
             for n, peer in enumerate(group):
-                send(gsend.at[1], grecv.at[3 + n], g_recv.at[3 + n], peer)
+                send(gsend.at[1], grecv.at[3 + n], g_recv.at[1], peer)
 
         def grad(j):
             inv = inv_ref[...]
@@ -346,16 +389,13 @@
                 send_copy(step[1])
             elif kind == "norm":
                 norm()
-                for j in range(features // LANES):
-                    at = slice(j * LANES, (j + 1) * LANES)
-                    gain_row[:, at] = gain_ref[at].reshape(1, -1)
             elif kind == "part":
                 block(*step[1:])
             elif kind == "W":
                 _, q, k, yy, h = step
                 got(step)
                 piece = w_piece(q, k, yy, h)
-                send(piece, piece, c_recv.at[q, k, yy, h], peer_c)
+                send(piece, piece, c_recv.at[k], peer_c)
             elif kind == "dot":
                 dots(*step[1:])
             elif kind == "gain":
@@ -368,8 +408,8 @@
             got(("fin", h))
             wg_ref[split(h), :] = (total + fin[split(h), :].astype(f32)) * grad_scale
         terms = [gsend[1]]
+        arrived(grecv.at[pl.ds(3, len(group))], g_recv.at[1], "g1")
         for n in range(3, 3 + len(group)):
-            arrived(grecv.at[n], g_recv.at[n], ("g", n))
             terms.append(grecv[n])
         while len(terms) > 1:
             terms = [terms[i] + terms[i + 1] for i in range(0, len(terms), 2)]
@@ -381,8 +421,7 @@
             copy.wait_send()
 
     steps = plan()
-    end = lax.rem(lax.div(z + 1, 2), 2) == 0
-    for name, here in (("E", end), ("I", jnp.logical_not(end))):
+    for name, here in (("E", end), ("I", inside)):
         pl.when(here)(functools.partial(role, name, steps[name]))
 
 
@@ -427,16 +466,15 @@
             pltpu.VMEM((n_tok, features), f32),
             pltpu.VMEM((n_z, 2, 2) + block, bf16),
             pltpu.VMEM((n_z, 2) + block, bf16),
-            pltpu.VMEM((n_z, 2) + block, bf16),
+            pltpu.VMEM((n_z - 1, 2) + block, bf16),
             pltpu.VMEM((2, 2) + block, bf16),
             pltpu.VMEM(block, bf16),
             pltpu.VMEM((2, 1, features), f32),
             pltpu.VMEM((2 * n_z + 2, 1, features), f32),
             pltpu.VMEM((1, features), f32),
-            dma((160,)),
-            dma((2, n_z, 2, HA)), dma((2, n_z, 2, HA)),
-            dma((n_z, 2, HR)), dma((n_z, 2, HR)), dma((2, 2, HR)), dma((HR,)),
-            dma((n_z, 2)), dma((2,)), dma((2 * n_z + 2,)),
+            dma, dma((2, n_z, 2, HA)), dma((n_z,)),
+            dma((n_z, 2, HR)), dma((n_z - 1, 2, HR)), dma((2, 2, HR)), dma((HR,)),
+            dma((n_z,)), dma, dma((2,)),
         ],
         compiler_params=pltpu.CompilerParams(
             collective_id=0, has_side_effects=True, vmem_limit_bytes=40 * 1024 * 1024
@@ -486,7 +524,7 @@
     n_z = n_grp // 2
     if (
         n_rep == 2 * 2 and n_grp == 2 * 4
-        and key_weight.shape[1] % (n_rep * LANES) == 0 and key_weight.shape[0] % 32 == 0
+        and key_weight.shape[1] % (n_rep * LANES) == 0 and key_weight.shape[0] % 96 == 0
         and tokens.shape[1] % (18 * LANES) == 0 and tokens.shape[0] % LANES == 0
     ):
         return fused(n_rep, n_grp, tokens, norm_gain, key_weight, key_grad)

time: 47 us -> 42.6 us (0.906)
  Pallas kernels: 46.1 us -> 41.6 us
    pallas_call x1, Pallas kernels: 44.9 us -> 40.5 us  [fused(): pl.pallas_call(functools.partial(kernel, n_z, grad_scale), out_shape=(jax...]
where the time goes in v3:
time: 42.6 us; the launch traced here: 42.4 us
  Pallas kernels  41.6 us (98%)
  between operations  0.8 us (2%)
    pallas_call x1, Pallas kernels, fused(): pl.pallas_call(functools.partial(kernel, n_z, grad_scale), out_shape=(jax...  40.5 us
    pallas_call x1, Pallas kernels, fused(): pl.pallas_call(drain, out_shape=tuple((jax.ShapeDtypeStruct(a.shape, a.dt...  1.13 us

profile of v3, /device:TPU:0, one launch (start us, length us, event | category | flops | bytes accessed | tf_op | source)
XLA Modules:
  0.0 42.4 jit_solution(10952990013999758476)
XLA Ops:
  0.6 40.5 %shard_map.67 = (bf16[256,2304]{1,0:T(8,128)(2,1)S(1)}, f32[288,256]{1,0:T(8,128)S(1)}, f32[2304]{0:T(1024)S(1)}) custom-call(bf16[256,2304]{1,0:T(8,128)(2,1)} %tok_hbm.1, f32[2304]{0:T(1024)} %gain_hbm.1, bf16[288,1024]{1,0:T(8,128)(2,1)} %w_hbm.1, bf16[256,1024]{1,0:T(8,128)(2,1)} %kg_hbm.1), custom_call_target="tpu_custom_call" | custom-call | tf_op jit(solution)/shard_map/pallas_call | solution.py:447
  41.1 1.1 %shard_map.68 = (bf16[256,2304]{1,0:T(8,128)(2,1)}, f32[288,256]{1,0:T(8,128)}, f32[2304]{0:T(1024)}) custom-call(bf16[256,2304]{1,0:T(8,128)(2,1)S(1)} %get-tuple-element.6.tg_ref, f32[288,256]{1,0:T(8,128)S(1)} %get-tuple-element.7.wg_ref, f32[2304]{0:T(1024)S(1)} %get-tuple-element.8.gg_ref), custom_call_target="tpu_custom_call" | custom-call | tf_op jit(solution)/shard_map/pallas_call | solution.py:483

commit v4 on v3

--- a/solution.py
+++ b/solution.py
@@ -24,7 +24,10 @@
 HA, HR = 2, 3
 PIECE, HOP, LEAD, AHEAD = 3.2, 2.5, 1.2, 11.0
 OWN, PART, STEP, GUARD = 0.4, 2.7, 0.45, 1.0
-XF = {(0, 0), (1, 0), (1, 1), (2, 0), (2, 1), (3, 0)}
+SECOND, CLEAR = 2.8, 0.8
+FAR, AGT, RST = 1.4, 1.0, 1.5
+XF = {(0, 0), (0, 1), (1, 0), (1, 1), (2, 0), (2, 1), (3, 0), (3, 1)}
+BY_Y = {"E": {(3, 0), (3, 1)}, "I": {(3, 0), (3, 1)}}
 PART_ORDER = [(3, 1), (2, 1), (2, 0), (3, 0), (0, 1), (1, 1), (1, 0), (0, 0)]
 
 
@@ -42,7 +45,10 @@
                     needs = ("own",) if k == me else ("W", q, k, 0, h)
                     if q == 0:
                         add(role, "y", ("W", q, k, 0, h), role, ("W", q, k, 1, h), [needs], size)
-                        add(role, "x", ("W", q, k, 1, h), role, ("W", 1, k, 1, h), [("W", 0, k, 1, h)], size)
+                        if (k, h) not in BY_Y[role]:
+                            add(role, "x", ("W", q, k, 1, h), role, ("W", 1, k, 1, h), [("W", 0, k, 1, h)], size)
+                    elif (k, h) in BY_Y[role]:
+                        add(role, "y", ("W", q, k, 0, h), role, ("W", 1, k, 1, h), [needs], size)
                     if role == "E" and k == 0:
                         add(role, "z", ("W", q, k, 0, h), "I", ("W", q, 0, 0, h), [needs], size)
                     if role == "I" and k >= 1:
@@ -86,7 +92,7 @@
     def tail(i):
         if i not in tails:
             copy = copies[i]
-            rest = AHEAD if copy["arrives"][0] == "W" else 1.5
+            rest = AHEAD if copy["arrives"][0] == "W" else RST
             for j in users.get((copy["dst"], copy["arrives"]), []):
                 rest = max(rest, tail(j))
             tails[i] = rest + copy["size"] + HOP
@@ -119,7 +125,7 @@
         got = [(t, what) for (r, what), t in known.items() if r == role and what[0] == "W"]
         near = max(t for t, what in got if what[2] < 2) + 2.0
         early = max(max(t for t, what in got if what[2] == 2) + 1.8, near + 1.5)
-        far = max(max(t for t, what in got) + 1.4, early + 0.5)
+        far = max(max(t for t, what in got) + FAR, early + 0.5)
         return got, near, early, far
 
     first = schedule(dict(known), {})
@@ -127,6 +133,7 @@
     for role in "EI":
         gain = marks(first, role)[3] + 1.1
         blocked[role, "x"] = (gain - GUARD, gain + 0.1)
+        blocked[role, "z"] = (gain + SECOND - CLEAR, gain + SECOND + 0.1)
     known = schedule(known, blocked)
     steps = {}
     for role in "EI":
@@ -141,15 +148,15 @@
             todo.append((far + 0.55 * (j - 1) if j else early, 3, ("dot", 1, j)))
         gain = marks(first, role)[3] + 1.1
         todo.append((gain, 3, ("gain", 1)))
-        last = max(copy["start"] for copy in copies if copy["role"] == role)
-        todo.append((max(far + 4.0, last - LEAD + 0.1), 3, ("gain", 2)))
+        todo.append((gain + SECOND, 3, ("gain", 2)))
         for j in range(3):
             todo.append((far + 1.7 + 0.2 * j, 4, ("grad", j)))
         for i, copy in enumerate(copies):
             if copy["role"] == role:
                 t = copy["start"] - LEAD
-                if copy["link"] == "x" and copy["start"] > gain:
-                    t = max(t, gain + 0.01)
+                for link, at in (("x", gain), ("z", gain + SECOND)):
+                    if copy["link"] == link and copy["start"] > at:
+                        t = max(t, at + 0.01 + copy["start"] / 1000)
                 t = 0.0 if copy["needs"] == [("own",)] and t < 1.0 else t
                 todo.append((max(copy["ready"], t), 5 + i, ("send", copy)))
         steps[role] = [step for _, _, step in sorted(todo, key=lambda a: a[:2])]
@@ -371,7 +378,7 @@
                 return
             arrived(grecv.at[pl.ds(0, 3)], g_recv.at[0], "g0")
             gsend[1] = (gsend[0] + grecv[0]) + (grecv[1] + grecv[2])
-            for n, peer in enumerate(group):
+            for n, peer in reversed(list(enumerate(group))):
                 send(gsend.at[1], grecv.at[3 + n], g_recv.at[1], peer)
 
         def grad(j):

time: 42.6 us -> 41.2 us (0.967)
  Pallas kernels: 41.6 us -> 40.2 us
    pallas_call x1, Pallas kernels: 40.5 us -> 39.1 us  [fused(): pl.pallas_call(functools.partial(kernel, n_z, grad_scale), out_shape=(jax...]
where the time goes in v4:
time: 41.2 us; the launch traced here: 41 us
  Pallas kernels  40.2 us (98%)
  between operations  0.8 us (2%)
    pallas_call x1, Pallas kernels, fused(): pl.pallas_call(functools.partial(kernel, n_z, grad_scale), out_shape=(jax...  39.1 us
    pallas_call x1, Pallas kernels, fused(): pl.pallas_call(drain, out_shape=tuple((jax.ShapeDtypeStruct(a.shape, a.dt...  1.13 us

profile of v4, /device:TPU:0, one launch (start us, length us, event | category | flops | bytes accessed | tf_op | source)
XLA Modules:
  0.0 41.0 jit_solution(5628356091994346200)
XLA Ops:
  0.6 39.1 %shard_map.67 = (bf16[256,2304]{1,0:T(8,128)(2,1)S(1)}, f32[288,256]{1,0:T(8,128)S(1)}, f32[2304]{0:T(1024)S(1)}) custom-call(bf16[256,2304]{1,0:T(8,128)(2,1)} %tok_hbm.1, f32[2304]{0:T(1024)} %gain_hbm.1, bf16[288,1024]{1,0:T(8,128)(2,1)} %w_hbm.1, bf16[256,1024]{1,0:T(8,128)(2,1)} %kg_hbm.1), custom_call_target="tpu_custom_call" | custom-call | tf_op jit(solution)/shard_map/pallas_call | solution.py:454
  39.7 1.1 %shard_map.68 = (bf16[256,2304]{1,0:T(8,128)(2,1)}, f32[288,256]{1,0:T(8,128)}, f32[2304]{0:T(1024)}) custom-call(bf16[256,2304]{1,0:T(8,128)(2,1)S(1)} %get-tuple-element.6.tg_ref, f32[288,256]{1,0:T(8,128)S(1)} %get-tuple-element.7.wg_ref, f32[2304]{0:T(1024)S(1)} %get-tuple-element.8.gg_ref), custom_call_target="tpu_custom_call" | custom-call | tf_op jit(solution)/shard_map/pallas_call | solution.py:490

commit v5 on v4

--- a/solution.py
+++ b/solution.py
@@ -23,8 +23,8 @@
 
 HA, HR = 2, 3
 PIECE, HOP, LEAD, AHEAD = 3.2, 2.5, 1.2, 11.0
-OWN, PART, STEP, GUARD = 0.4, 2.7, 0.45, 1.0
-SECOND, CLEAR = 2.8, 0.8
+OWN, PART, STEP, GUARD = 0.4, 2.7, 0.45, 0.6
+SECOND, CLEAR, EDGE = 2.8, 0.4, 2.0
 FAR, AGT, RST = 1.4, 1.0, 1.5
 XF = {(0, 0), (0, 1), (1, 0), (1, 1), (2, 0), (2, 1), (3, 0), (3, 1)}
 BY_Y = {"E": {(3, 0), (3, 1)}, "I": {(3, 0), (3, 1)}}
@@ -92,7 +92,7 @@
     def tail(i):
         if i not in tails:
             copy = copies[i]
-            rest = AHEAD if copy["arrives"][0] == "W" else RST
+            rest = {"W": AHEAD, "fin": RST + (EDGE if copy["dst"] == "E" else 0.0)}.get(copy["arrives"][0], RST)
             for j in users.get((copy["dst"], copy["arrives"]), []):
                 rest = max(rest, tail(j))
             tails[i] = rest + copy["size"] + HOP
@@ -201,7 +201,7 @@
             ((w_hbm, wfull.at[own_rows, :]), (tok_hbm, tok_ref), (kg_hbm, kg_ref), (gain_hbm, gain_ref))
         )
     ]
-    for load in loads:
+    for load in (loads[1], loads[0], loads[2], loads[3]):
         load.start()
 
     end = lax.rem(lax.div(z + 1, 2), 2) == 0

time: 41.2 us -> 41 us (level)
  no operation moved by 1% of the time
where the time goes in v5:
time: 41 us; the launch traced here: 40.9 us
  Pallas kernels  40.1 us (98%)
  between operations  0.8 us (2%)
    pallas_call x1, Pallas kernels, fused(): pl.pallas_call(functools.partial(kernel, n_z, grad_scale), out_shape=(jax...  39 us
    pallas_call x1, Pallas kernels, fused(): pl.pallas_call(drain, out_shape=tuple((jax.ShapeDtypeStruct(a.shape, a.dt...  1.13 us

profile of v5, /device:TPU:0, one launch (start us, length us, event | category | flops | bytes accessed | tf_op | source)
XLA Modules:
  0.0 40.9 jit_solution(16142860072582606487)
XLA Ops:
  0.6 39.0 %shard_map.67 = (bf16[256,2304]{1,0:T(8,128)(2,1)S(1)}, f32[288,256]{1,0:T(8,128)S(1)}, f32[2304]{0:T(1024)S(1)}) custom-call(bf16[256,2304]{1,0:T(8,128)(2,1)} %tok_hbm.1, f32[2304]{0:T(1024)} %gain_hbm.1, bf16[288,1024]{1,0:T(8,128)(2,1)} %w_hbm.1, bf16[256,1024]{1,0:T(8,128)(2,1)} %kg_hbm.1), custom_call_target="tpu_custom_call" | custom-call | tf_op jit(solution)/shard_map/pallas_call | solution.py:454
  39.6 1.1 %shard_map.68 = (bf16[256,2304]{1,0:T(8,128)(2,1)}, f32[288,256]{1,0:T(8,128)}, f32[2304]{0:T(1024)}) custom-call(bf16[256,2304]{1,0:T(8,128)(2,1)S(1)} %get-tuple-element.6.tg_ref, f32[288,256]{1,0:T(8,128)S(1)} %get-tuple-element.7.wg_ref, f32[2304]{0:T(1024)S(1)} %get-tuple-element.8.gg_ref), custom_call_target="tpu_custom_call" | custom-call | tf_op jit(solution)/shard_map/pallas_call | solution.py:490
